TPU v7x, 32 devices: a whole 2x2x4 slice. The times are simulated.
32 devices in a mesh: dp: 8 (over z, x), tensor: 4 (over y, core).
Axes of the slice: x: 2, y: 2, z: 4, core: 2. Of those that a mesh axis runs over, the one named last changes fastest.
Arguments:
- tokens: bfloat16 [2, 8, 1024, 1024], P(None, 'dp', 'tensor'), may hold values from -6 to 6
- segment_ids: int32 [2, 8, 1024], P(None, 'dp'), may hold values from 0 to 2, as said below
- attn_gain: float32 [1024], replicated, may hold values from 0.1 to 1.9
- query_gain: float32 [64], replicated, may hold values from 0.1 to 1.9
- key_gain: float32 [64], replicated, may hold values from 0.1 to 1.9
- w_query: bfloat16 [1024, 1024], P('dp', 'tensor'), may hold values from -0.1875 to 0.1875
- w_key: bfloat16 [1024, 512], P('dp', 'tensor'), may hold values from -0.1875 to 0.1875
- w_value: bfloat16 [1024, 512], P('dp', 'tensor'), may hold values from -0.1875 to 0.1875
- w_out: bfloat16 [1024, 1024], P('tensor', 'dp'), may hold values from -1.5 to 1.5
- ffn_gain: float32 [1024], replicated, may hold values from 0.1 to 1.9
- w_gate: bfloat16 [1024, 4608], P('dp', 'tensor'), may hold values from -0.1875 to 0.1875
- w_up: bfloat16 [1024, 4608], P('dp', 'tensor'), may hold values from -0.1875 to 0.1875
- w_down: bfloat16 [4608, 1024], P('tensor', 'dp'), may hold values from -0.09375 to 0.09375
- cotangent: bfloat16 [2, 8, 1024, 1024], P(None, 'dp', 'tensor'), may hold values from -6 to 6
Outputs:
- mixed: bfloat16 [2, 8, 1024, 1024], P(None, 'dp', 'tensor')
- grad_tokens: float32 [2, 8, 1024, 1024], P(None, 'dp', 'tensor')
- grad_attn_gain: float32 [1024], replicated
- grad_query_gain: float32 [64], replicated
- grad_key_gain: float32 [64], replicated
- grad_query: float32 [1024, 1024], P('dp', 'tensor')
- grad_key: float32 [1024, 512], P('dp', 'tensor')
- grad_value: float32 [1024, 512], P('dp', 'tensor')
- grad_out: float32 [1024, 1024], P('tensor', 'dp')
- grad_ffn_gain: float32 [1024], replicated
- grad_gate: float32 [1024, 4608], P('dp', 'tensor')
- grad_up: float32 [1024, 4608], P('dp', 'tensor')
- grad_down: float32 [4608, 1024], P('tensor', 'dp')
Inputs may be any that keep to these rules, and one draw needn't show every extreme that they name: `segment_ids`: ids never fall along a sequence and every sequence holds documents 0, 1 and 2; document 0 has 204 to 408 tokens, document 1 has 204 to 511 tokens.
All inputs are finite; a program needn't handle non-finite values.
Results may differ from a plain program's by a relative error of at most 0.017.
Values may be sent and summed in bfloat16 or wider, within the bound.
A program may use at most 112 MiB of HBM per device.

v0:
```python
import jax
import jax.numpy as jnp
from jax import lax
from jax.sharding import PartitionSpec as P

D = 1024
DH = 64
BLOCK = 512


NORM_EPS = 1e-05
ROPE_BASE = 1000000.0


def rope_tables(length, head_width):
    freq_index = jnp.arange(head_width // 2, dtype=jnp.float32)
    inverse_freq = ROPE_BASE ** (-2.0 * freq_index / head_width)
    angles = jnp.arange(length, dtype=jnp.float32)[:, None] * inverse_freq[None, :]
    return (jnp.cos(angles), jnp.sin(angles))


def rotate(values, cosine_table, sine_table):
    half_width = values.shape[-1] // 2
    front_half = values[..., :half_width]
    back_half = values[..., half_width:]
    return jnp.concatenate(
        [
            front_half * cosine_table - back_half * sine_table,
            back_half * cosine_table + front_half * sine_table,
        ],
        axis=-1,
    )


def norm_forward(values, gain_vector):
    inverse = lax.rsqrt(jnp.mean(values * values, axis=-1, keepdims=True) + NORM_EPS)
    return (values * inverse * gain_vector, inverse)


def norm_backward(values, inverse, gain_vector, upstream):
    scaled = values * inverse
    weighted = upstream * gain_vector
    back_grad = inverse * (weighted - scaled * jnp.mean(weighted * scaled, axis=-1, keepdims=True))
    return (back_grad, upstream * scaled)


def product(left_side, right_side):
    return jnp.dot(left_side, right_side, preferred_element_type=jnp.float32)


def times_transposed(left_side, right_side):
    return lax.dot_general(
        left_side, right_side, (((1,), (1,)), ((), ())), preferred_element_type=jnp.float32
    )


def transposed_times(left_side, right_side):
    return lax.dot_general(
        left_side, right_side, (((0,), (0,)), ((), ())), preferred_element_type=jnp.float32
    )


def shards(
    tokens,
    segment_ids,
    attn_gain,
    query_gain,
    key_gain,
    w_query,
    w_key,
    w_value,
    w_out,
    ffn_gain,
    w_gate,
    w_up,
    w_down,
    cotangent,
):
    micro_count = tokens.shape[0]
    length = segment_ids.shape[2]
    block_count = length // BLOCK
    head_count = w_query.shape[1] // DH
    group_count = w_key.shape[1] // DH
    group_size = head_count // group_count
    score_scale = DH ** (-0.5)
    cosine_table, sine_table = rope_tables(length, DH)
    cosine_heads = cosine_table[:, None, :]
    sine_heads = sine_table[:, None, :]
    positions = jnp.arange(length)
    attn_kept = (
        lax.all_gather(w_query, "dp", axis=0, tiled=True),
        lax.all_gather(w_key, "dp", axis=0, tiled=True),
        lax.all_gather(w_value, "dp", axis=0, tiled=True),
        lax.all_gather(w_out, "dp", axis=1, tiled=True),
    )
    ffn_kept = (
        lax.all_gather(w_gate, "dp", axis=0, tiled=True),
        lax.all_gather(w_up, "dp", axis=0, tiled=True),
        lax.all_gather(w_down, "dp", axis=1, tiled=True),
    )

    def attn_source():
        return attn_kept

    def ffn_source():
        return ffn_kept

    def heads_major(values):
        return values.reshape(length, group_count, group_size, DH).transpose(1, 2, 0, 3)

    def block_mask(block_index, segments):
        row_start = block_index * BLOCK
        row_end = row_start + BLOCK
        row_pos = positions[row_start:row_end]
        return (row_pos[:, None] >= positions[None, :row_end]) & (
            segments[row_start:row_end, None] == segments[None, :row_end]
        )

    def attention_backward(query_major, key_major, value_major, log_totals, grad_major, segments):
        query_grads = []
        key_grad = jnp.zeros((group_count, length, DH), jnp.float32)
        value_grad = jnp.zeros((group_count, length, DH), jnp.float32)
        for block_index in range(block_count):
            row_start = block_index * BLOCK
            row_end = row_start + BLOCK
            query_block = query_major[:, :, row_start:row_end]
            grad_block = grad_major[:, :, row_start:row_end]
            allowed = block_mask(block_index, segments)
            scores = jnp.einsum(
                "gjqd,gkd->gjqk",
                query_block,
                key_major[:, :row_end],
                preferred_element_type=jnp.float32,
            )
            probabilities = jnp.where(allowed, jnp.exp(scores - log_totals[block_index]), 0.0)
            prob_grad = jnp.einsum(
                "gjqd,gkd->gjqk",
                grad_block,
                value_major[:, :row_end],
                preferred_element_type=jnp.float32,
            )
            row_delta = jnp.sum(probabilities * prob_grad, axis=-1, keepdims=True)
            score_grad = (probabilities * (prob_grad - row_delta)).astype(jnp.bfloat16)
            query_grads.append(
                jnp.einsum(
                    "gjqk,gkd->gjqd",
                    score_grad,
                    key_major[:, :row_end],
                    preferred_element_type=jnp.float32,
                )
            )
            key_part = jnp.einsum(
                "gjqk,gjqd->gkd", score_grad, query_block, preferred_element_type=jnp.float32
            )
            value_part = jnp.einsum(
                "gjqk,gjqd->gkd",
                probabilities.astype(jnp.bfloat16),
                grad_block,
                preferred_element_type=jnp.float32,
            )
            key_grad = key_grad.at[:, :row_end].add(key_part)
            value_grad = value_grad.at[:, :row_end].add(value_part)
        query_grad_all = (
            jnp.concatenate(query_grads, axis=2)
            .transpose(2, 0, 1, 3)
            .reshape(length, head_count, DH)
        )
        return (query_grad_all, key_grad.transpose(1, 0, 2), value_grad.transpose(1, 0, 2))

    grad_accs = (
        jnp.zeros((D, w_query.shape[1]), jnp.float32),
        jnp.zeros((D, w_key.shape[1]), jnp.float32),
        jnp.zeros((D, w_value.shape[1]), jnp.float32),
        jnp.zeros((w_out.shape[0], D), jnp.float32),
        jnp.zeros((D, w_gate.shape[1]), jnp.float32),
        jnp.zeros((D, w_up.shape[1]), jnp.float32),
        jnp.zeros((w_down.shape[0], D), jnp.float32),
    )
    shard_sums = None
    attn_gain_acc = jnp.zeros((D,), jnp.float32)
    ffn_gain_acc = jnp.zeros((D,), jnp.float32)
    query_gain_acc = jnp.zeros((DH,), jnp.float32)
    key_gain_acc = jnp.zeros((DH,), jnp.float32)
    mixed_rows = []
    input_grads = []
    for micro_index in range(micro_count):
        rows_in = tokens[micro_index, 0].astype(jnp.float32)
        segments = segment_ids[micro_index, 0]
        query_full, key_full, value_full, out_full = attn_source()
        normed, inverse_one = norm_forward(rows_in, attn_gain)
        normed_all = lax.all_gather(normed.astype(jnp.bfloat16), "tensor", axis=0, tiled=True)
        query_heads = product(normed_all, query_full).reshape(length, head_count, DH)
        key_heads = product(normed_all, key_full).reshape(length, group_count, DH)
        value_low = (
            product(normed_all, value_full).astype(jnp.bfloat16).reshape(length, group_count, DH)
        )
        query_normed, query_inverse = norm_forward(query_heads, query_gain)
        query_rot = (rotate(query_normed, cosine_heads, sine_heads) * score_scale).astype(
            jnp.bfloat16
        )
        key_normed, key_inverse = norm_forward(key_heads, key_gain)
        key_rot = rotate(key_normed, cosine_heads, sine_heads).astype(jnp.bfloat16)
        query_major = heads_major(query_rot)
        key_major = key_rot.transpose(1, 0, 2)
        value_major = value_low.transpose(1, 0, 2)
        outputs = []
        attention_log_totals = []
        for attention_block_index in range(block_count):
            attention_row_start = attention_block_index * BLOCK
            attention_row_end = attention_row_start + BLOCK
            attention_query_block = query_major[:, :, attention_row_start:attention_row_end]
            attention_allowed = block_mask(attention_block_index, segments)
            attention_scores = jnp.einsum(
                "gjqd,gkd->gjqk",
                attention_query_block,
                key_major[:, :attention_row_end],
                preferred_element_type=jnp.float32,
            )
            attention_scores = jnp.where(attention_allowed, attention_scores, -1e30)
            row_top = jnp.max(attention_scores, axis=-1, keepdims=True)
            weights = jnp.exp(attention_scores - row_top)
            row_total = jnp.sum(weights, axis=-1, keepdims=True)
            attention_probabilities = (weights / row_total).astype(jnp.bfloat16)
            outputs.append(
                jnp.einsum(
                    "gjqk,gkd->gjqd",
                    attention_probabilities,
                    value_major[:, :attention_row_end],
                    preferred_element_type=jnp.float32,
                )
            )
            attention_log_totals.append(row_top + jnp.log(row_total))
        attended = (
            jnp.concatenate(outputs, axis=2).transpose(2, 0, 1, 3).reshape(length, head_count * DH)
        )
        log_totals = attention_log_totals
        attended_low = attended.astype(jnp.bfloat16)
        branch = lax.psum_scatter(
            product(attended_low, out_full), "tensor", scatter_dimension=0, tiled=True
        )
        middle = rows_in + branch
        ffn_normed, inverse_two = norm_forward(middle, ffn_gain)
        ffn_all = lax.all_gather(ffn_normed.astype(jnp.bfloat16), "tensor", axis=0, tiled=True)
        gate_full, up_full, down_full = ffn_source()
        gate_proj = product(ffn_all, gate_full)
        up_proj = product(ffn_all, up_full)
        gate_sig = jax.nn.sigmoid(gate_proj)
        gate_act = gate_proj * gate_sig
        hidden = (gate_act * up_proj).astype(jnp.bfloat16)
        ffn_out = lax.psum_scatter(
            product(hidden, down_full).astype(jnp.bfloat16),
            "tensor",
            scatter_dimension=0,
            tiled=True,
        ).astype(jnp.float32)
        mixed_rows.append((middle + ffn_out).astype(jnp.bfloat16))
        upstream = cotangent[micro_index, 0].astype(jnp.float32)
        gate_full, up_full, down_full = ffn_source()
        ffn_upstream = lax.all_gather(upstream.astype(jnp.bfloat16), "tensor", axis=0, tiled=True)
        hidden_grad = times_transposed(ffn_upstream, down_full)
        gate_grad = (
            hidden_grad * up_proj * gate_sig * (1.0 + gate_proj * (1.0 - gate_sig))
        ).astype(jnp.bfloat16)
        up_grad = (hidden_grad * gate_act).astype(jnp.bfloat16)
        ffn_part = times_transposed(gate_grad, gate_full) + times_transposed(up_grad, up_full)
        ffn_normed_grad = lax.psum_scatter(
            ffn_part.astype(jnp.bfloat16), "tensor", scatter_dimension=0, tiled=True
        ).astype(jnp.float32)
        middle_back, ffn_term = norm_backward(middle, inverse_two, ffn_gain, ffn_normed_grad)
        ffn_gain_acc = ffn_gain_acc + jnp.sum(ffn_term, axis=0)
        middle_grad = upstream + middle_back
        attn_upstream = lax.all_gather(
            middle_grad.astype(jnp.bfloat16), "tensor", axis=0, tiled=True
        )
        query_full, key_full, value_full, out_full = attn_source()
        attended_grad = times_transposed(attn_upstream, out_full).astype(jnp.bfloat16)
        rot_query_grad, key_rot_grad, value_grad = attention_backward(
            query_major, key_major, value_major, log_totals, heads_major(attended_grad), segments
        )
        query_normed_grad = rotate(rot_query_grad * score_scale, cosine_heads, -sine_heads)
        query_back, query_term = norm_backward(
            query_heads, query_inverse, query_gain, query_normed_grad
        )
        query_gain_acc = query_gain_acc + jnp.sum(query_term, axis=(0, 1))
        query_grad = query_back.reshape(length, head_count * DH).astype(jnp.bfloat16)
        key_normed_grad = rotate(key_rot_grad, cosine_heads, -sine_heads)
        key_back, key_term = norm_backward(key_heads, key_inverse, key_gain, key_normed_grad)
        key_gain_acc = key_gain_acc + jnp.sum(key_term, axis=(0, 1))
        key_grad = key_back.reshape(length, group_count * DH).astype(jnp.bfloat16)
        value_grad_low = value_grad.reshape(length, group_count * DH).astype(jnp.bfloat16)
        attn_part = (
            times_transposed(query_grad, query_full)
            + times_transposed(key_grad, key_full)
            + times_transposed(value_grad_low, value_full)
        )
        normed_grad = lax.psum_scatter(
            attn_part.astype(jnp.bfloat16), "tensor", scatter_dimension=0, tiled=True
        ).astype(jnp.float32)
        token_back, attn_term = norm_backward(rows_in, inverse_one, attn_gain, normed_grad)
        attn_gain_acc = attn_gain_acc + jnp.sum(attn_term, axis=0)
        input_grads.append(middle_grad + token_back)
        grad_accs = (
            grad_accs[0] + transposed_times(normed_all, query_grad),
            grad_accs[1] + transposed_times(normed_all, key_grad),
            grad_accs[2] + transposed_times(normed_all, value_grad_low),
            grad_accs[3] + transposed_times(attended_low, attn_upstream),
            grad_accs[4] + transposed_times(ffn_all, gate_grad),
            grad_accs[5] + transposed_times(ffn_all, up_grad),
            grad_accs[6] + transposed_times(hidden, ffn_upstream),
        )
    shard_sums = (
        lax.psum_scatter(grad_accs[0], "dp", scatter_dimension=0, tiled=True),
        lax.psum_scatter(grad_accs[1], "dp", scatter_dimension=0, tiled=True),
        lax.psum_scatter(grad_accs[2], "dp", scatter_dimension=0, tiled=True),
        lax.psum_scatter(grad_accs[3], "dp", scatter_dimension=1, tiled=True),
        lax.psum_scatter(grad_accs[4], "dp", scatter_dimension=0, tiled=True),
        lax.psum_scatter(grad_accs[5], "dp", scatter_dimension=0, tiled=True),
        lax.psum_scatter(grad_accs[6], "dp", scatter_dimension=1, tiled=True),
    )
    gain_sums = lax.psum(
        (attn_gain_acc, query_gain_acc, key_gain_acc, ffn_gain_acc), ("dp", "tensor")
    )
    mixed = jnp.stack(mixed_rows, axis=0)[:, None]
    grad_tokens = jnp.stack(input_grads, axis=0)[:, None]
    return (
        mixed,
        grad_tokens,
        gain_sums[0],
        gain_sums[1],
        gain_sums[2],
        shard_sums[0],
        shard_sums[1],
        shard_sums[2],
        shard_sums[3],
        gain_sums[3],
        shard_sums[4],
        shard_sums[5],
        shard_sums[6],
    )


def solution(mesh):
    placed = (
        P(None, "dp", "tensor", None),
        P(None, "dp", None),
        P(),
        P(),
        P(),
        P("dp", "tensor"),
        P("dp", "tensor"),
        P("dp", "tensor"),
        P("tensor", "dp"),
        P(),
        P("dp", "tensor"),
        P("dp", "tensor"),
        P("tensor", "dp"),
        P(None, "dp", "tensor", None),
    )
    return jax.shard_map(
        shards,
        mesh=mesh,
        in_specs=placed,
        out_specs=(
            P(None, "dp", "tensor", None),
            P(None, "dp", "tensor", None),
            P(),
            P(),
            P(),
            P("dp", "tensor"),
            P("dp", "tensor"),
            P("dp", "tensor"),
            P("tensor", "dp"),
            P(),
            P("dp", "tensor"),
            P("dp", "tensor"),
            P("tensor", "dp"),
        ),
        check_vma=False,
    )
```

profile of v0, /device:TPU:0, one launch (start us, length us, event | category | flops | bytes accessed | tf_op | source)
XLA Modules:
  0.0 1374.8 jit_solution(15350774475593715328)
XLA Ops:
  13.5 32.7 %all_gather.47 = bf16[1024,128]{1,0:T(8,128)(2,1)S(1)} all-gather(bf16[128,128]{1,0:T(8,128)(2,1)S(1)} %copy-done.111), channel_id=1, replica_groups=mesh['dp'=8,'tensor'=4] {'dp'}, dimensions={0}, use_global_device_ids=true | all-gather | bytes 294912 | tf_op jit(solution)/shard_map/all_gather | solution.py:92
  46.2 32.8 %all_gather.48 = bf16[1024,128]{1,0:T(8,128)(2,1)} all-gather(bf16[128,128]{1,0:T(8,128)(2,1)S(1)} %copy-done.112), channel_id=1, replica_groups=mesh['dp'=8,'tensor'=4] {'dp'}, dimensions={0}, use_global_device_ids=true | all-gather | bytes 294912 | tf_op jit(solution)/shard_map/all_gather | solution.py:93
  79.1 33.7 %all_gather.46 = bf16[1024,256]{1,0:T(8,128)(2,1)} all-gather(bf16[128,256]{1,0:T(8,128)(2,1)S(1)} %copy-done.104), channel_id=1, replica_groups=mesh['dp'=8,'tensor'=4] {'dp'}, dimensions={0}, use_global_device_ids=true | all-gather | bytes 589824 | tf_op jit(solution)/shard_map/all_gather | solution.py:91
  112.7 28.1 %all_gather.49 = bf16[256,1024]{1,0:T(8,128)(2,1)} all-gather(bf16[256,128]{1,0:T(8,128)(2,1)S(1)} %copy-done.105), channel_id=1, replica_groups=mesh['dp'=8,'tensor'=4] {'dp'}, dimensions={1}, use_global_device_ids=true | all-gather | bytes 589824 | tf_op jit(solution)/shard_map/all_gather | solution.py:94
  144.5 3.6 multiply_reduce_fusion.12
  190.9 26.7 %reduce-scatter.20.cloned.1.call-done = f32[256,1024]{1,0:T(8,128)} async-done(((f32[1024,1024]{1,0:T(8,128)}), f32[256,1024]{1,0:T(8,128)}) %reduce-scatter.20.cloned.1.call-update) | async-done | bytes 1048592 | tf_op jit(solution)/shard_map/reduce_scatter | solution.py:238
  217.6 47.0 %reduce-scatter.16.cloned.1.call-done = f32[256,1024]{1,0:T(8,128)} async-done(((f32[1024,1024]{1,0:T(8,128)}), f32[256,1024]{1,0:T(8,128)}) %reduce-scatter.16.cloned.1.call-update) | async-done | bytes 1048592 | tf_op jit(solution)/shard_map/reduce_scatter | solution.py:238
  271.8 18.4 %all-gather.16.cloned.1.call-done = bf16[1024,1024]{1,0:T(8,128)(2,1)} async-done(((bf16[256,1024]{1,0:T(8,128)(2,1)}), bf16[1024,1024]{1,0:T(8,128)(2,1)}) %all-gather.16.cloned.1.call-update) | async-done | bytes 2097168 | tf_op jit(solution)/shard_map/all_gather | solution.py:243
  290.2 7.3 fusion.176
  297.5 46.4 %all-gather.20.cloned.1.call-done = bf16[1024,1152]{1,0:T(8,128)(2,1)} async-done(((bf16[128,1152]{1,0:T(8,128)(2,1)}), bf16[1024,1152]{1,0:T(8,128)(2,1)}) %all-gather.20.cloned.1.call-update) | async-done | bytes 2359312 | tf_op jit(solution)/shard_map/all_gather | solution.py:98
  344.0 7.4 fusion.177
  351.3 15.7 %all-gather.32.cloned.1.call-done = bf16[1,1,1024,1024]{3,2,1,0:T(8,128)(2,1)} async-done(((bf16[1,1,256,1024]{3,2,1,0:T(8,128)(2,1)}), bf16[1,1,1024,1024]{3,2,1,0:T(8,128)(2,1)}) %all-gather.32.cloned.1.call-update) | async-done | bytes 2097168 | tf_op jit(solution)/shard_map/all_gather | solution.py:259
  367.1 55.4 %all-gather.22.cloned.1.call-done = bf16[1152,1024]{1,0:T(8,128)(2,1)} async-done(((bf16[1152,128]{1,0:T(8,128)(2,1)}), bf16[1152,1024]{1,0:T(8,128)(2,1)}) %all-gather.22.cloned.1.call-update) | async-done | bytes 2359312 | tf_op jit(solution)/shard_map/all_gather | solution.py:99
  422.5 10.8 multiply_convert_fusion.4
  436.7 4.1 add_convert_fusion.3
  440.9 29.3 %reduce-scatter.24.cloned.1.call-done = bf16[256,1024]{1,0:T(8,128)(2,1)} async-done(((bf16[1024,1024]{1,0:T(8,128)(2,1)}), bf16[256,1024]{1,0:T(8,128)(2,1)}) %reduce-scatter.24.cloned.1.call-update) | async-done | bytes 524304 | tf_op jit(solution)/shard_map/reduce_scatter | solution.py:266
  474.0 21.7 %all-gather.26.cloned.1.call-done = bf16[1024,1024]{1,0:T(8,128)(2,1)} async-done(((bf16[256,1024]{1,0:T(8,128)(2,1)}), bf16[1024,1024]{1,0:T(8,128)(2,1)}) %all-gather.26.cloned.1.call-update) | async-done | bytes 2097168 | tf_op jit(solution)/shard_map/all_gather | solution.py:243
  495.7 7.5 fusion.179
  503.2 4.5 fusion.180
  507.7 11.8 all-gather.34.cloned.1.call-done
  519.6 10.8 multiply_convert_fusion.2
  533.7 4.1 add_convert_fusion.1
  537.9 6.6 convolution_convert_fusion
  544.9 24.3 %reduce-scatter.28.cloned.1.call-done = bf16[256,1024]{1,0:T(8,128)(2,1)} async-done(((bf16[1024,1024]{1,0:T(8,128)(2,1)}), bf16[256,1024]{1,0:T(8,128)(2,1)}) %reduce-scatter.28.cloned.1.call-update) | async-done | bytes 524304 | tf_op jit(solution)/shard_map/reduce_scatter | solution.py:266
  570.7 32.1 %reduce-scatter.22.cloned.1.call-done = bf16[256,1024]{1,0:T(8,128)(2,1)} async-done(((bf16[1024,1024]{1,0:T(8,128)(2,1)}), bf16[256,1024]{1,0:T(8,128)(2,1)}) %reduce-scatter.22.cloned.1.call-update) | async-done | bytes 524304 | tf_op jit(solution)/shard_map/reduce_scatter | solution.py:250
  602.8 3.1 fusion.170
  607.0 21.4 %all-gather.30.cloned.1.call-done = bf16[1024,1024]{1,0:T(8,128)(2,1)} async-done(((bf16[256,1024]{1,0:T(8,128)(2,1)}), bf16[1024,1024]{1,0:T(8,128)(2,1)}) %all-gather.30.cloned.1.call-update) | async-done | bytes 2097168 | tf_op jit(solution)/shard_map/all_gather | solution.py:272
  633.1 3.2 multiply_reduce_fusion.2
  636.3 16.8 %all-gather.28.cloned.1.call-done = bf16[1024,1024]{1,0:T(8,128)(2,1)} async-done(((bf16[256,1024]{1,0:T(8,128)(2,1)}), bf16[1024,1024]{1,0:T(8,128)(2,1)}) %all-gather.28.cloned.1.call-update) | async-done | bytes 2097168 | tf_op jit(solution)/shard_map/all_gather | solution.py:272
  658.1 4.4 multiply_convert_fusion.8
  667.4 5.2 multiply_reduce_fusion
  675.1 5.1 multiply_reduce_fusion.1
  680.2 8.8 multiply_convert_fusion
  714.7 6.7 convolution_convert_fusion.1
  729.5 5.4 fusion.192
  734.9 4.7 convolution_add_fusion.1
  739.7 5.4 fusion.191
  745.2 4.8 convolution_add_fusion.2
  759.6 4.5 fusion.21
  764.2 4.4 convolution_add_fusion
  771.8 39.4 %all-reduce.4 = (f32[1024]{0:T(1024)}, f32[64]{0:T(128)}, f32[64]{0:T(128)}, f32[1024]{0:T(1024)}) all-reduce(f32[1024]{0:T(1024)S(1)} %add.351, f32[64]{0:T(128)S(1)} %add.352, f32[64]{0:T(128)S(1)} %add.353, f32[1024]{0:T(1024)S(1)} %add.358), channel_id=1, replica_groups=mesh['dp'=8,'tensor'=4] {'dp','tensor'}, use_global_device_ids=true, to_apply=%region_38.39 | all-reduce | flops 2176 | bytes 17408 | tf_op jit(solution)/shard_map/psum | solution.py:320
  816.7 52.4 %reduce-scatter.36.cloned.1.call-done = f32[128,128]{1,0:T(8,128)} async-done(((f32[1024,128]{1,0:T(8,128)}), f32[128,128]{1,0:T(8,128)}) %reduce-scatter.36.cloned.1.call-update) | async-done | bytes 65552 | tf_op jit(solution)/shard_map/reduce_scatter | solution.py:314
  869.1 65.6 %reduce-scatter.34.cloned.1.call-done = f32[128,128]{1,0:T(8,128)} async-done(((f32[1024,128]{1,0:T(8,128)}), f32[128,128]{1,0:T(8,128)}) %reduce-scatter.34.cloned.1.call-update) | async-done | bytes 65552 | tf_op jit(solution)/shard_map/reduce_scatter | solution.py:313
  934.7 98.7 %reduce-scatter.42.cloned.1.call-done = f32[128,1152]{1,0:T(8,128)} async-done(((f32[1024,1152]{1,0:T(8,128)}), f32[128,1152]{1,0:T(8,128)}) %reduce-scatter.42.cloned.1.call-update) | async-done | bytes 589840 | tf_op jit(solution)/shard_map/reduce_scatter | solution.py:317
  1033.4 99.5 %reduce-scatter.40.cloned.1.call-done = f32[128,1152]{1,0:T(8,128)} async-done(((f32[1024,1152]{1,0:T(8,128)}), f32[128,1152]{1,0:T(8,128)}) %reduce-scatter.40.cloned.1.call-update) | async-done | bytes 589840 | tf_op jit(solution)/shard_map/reduce_scatter | solution.py:316
  1132.9 68.3 %reduce-scatter.38.cloned.1.call-done = f32[256,128]{1,0:T(8,128)} async-done(((f32[256,1024]{1,0:T(8,128)}), f32[256,128]{1,0:T(8,128)}) %reduce-scatter.38.cloned.1.call-update) | async-done | bytes 131088 | tf_op jit(solution)/shard_map/reduce_scatter | solution.py:315
  1201.2 67.1 %reduce-scatter.32.cloned.1.call-done = f32[128,256]{1,0:T(8,128)} async-done(((f32[1024,256]{1,0:T(8,128)}), f32[128,256]{1,0:T(8,128)}) %reduce-scatter.32.cloned.1.call-update) | async-done | bytes 131088 | tf_op jit(solution)/shard_map/reduce_scatter | solution.py:312
  1268.3 99.1 %reduce-scatter.44.cloned.1.call-done = f32[1152,128]{1,0:T(8,128)} async-done(((f32[1152,1024]{1,0:T(8,128)}), f32[1152,128]{1,0:T(8,128)}) %reduce-scatter.44.cloned.1.call-update) | async-done | bytes 589840 | tf_op jit(solution)/shard_map/reduce_scatter | solution.py:318
  (487 shorter events, 139.9 us)
Async XLA Ops:
  8.0 38.2 %copy-start.112 = (bf16[128,128]{1,0:T(8,128)(2,1)S(1)}, bf16[128,128]{1,0:T(8,128)(2,1)}, u32[]{:S(2)}) copy-start(bf16[128,128]{1,0:T(8,128)(2,1)} %param.45) | copy-start | bytes 98308
  8.0 71.0 %copy-start.113 = (s32[2,1,1024]{2,1,0:T(1,128)S(1)}, s32[2,1,1024]{2,1,0:T(1,128)}, u32[]{:S(2)}) copy-start(s32[2,1,1024]{2,1,0:T(1,128)} %param.39) | copy-start | bytes 24580
  8.0 71.0 %copy-start.104 = (bf16[128,256]{1,0:T(8,128)(2,1)S(1)}, bf16[128,256]{1,0:T(8,128)(2,1)}, u32[]{:S(2)}) copy-start(bf16[128,256]{1,0:T(8,128)(2,1)} %param.43) | copy-start | bytes 196612
  8.1 104.7 %copy-start.105 = (bf16[256,128]{1,0:T(8,128)(2,1)S(1)}, bf16[256,128]{1,0:T(8,128)(2,1)}, u32[]{:S(2)}) copy-start(bf16[256,128]{1,0:T(8,128)(2,1)} %param.46) | copy-start | bytes 196612
  8.1 136.4 %all-gather.24.cloned.1.call-start = ((), (), s32[]{:S(2)}) async-start(), calls=%async_computation.22 | async-start | bytes 2621440 | tf_op jit(solution)/shard_map/all_gather | solution.py:191
  12.7 135.5 %all-gather.14.cloned.1.call-start = ((), (), s32[]{:S(2)}) async-start(), calls=%async_computation.15 | async-start | bytes 2621440 | tf_op jit(solution)/shard_map/all_gather | solution.py:191
  13.4 204.2 %reduce-scatter.20.cloned.1.call-start = ((), (), s32[]{:S(2)}) async-start(), calls=%async_computation.23 | async-start | bytes 5242880 | tf_op jit(solution)/shard_map/reduce_scatter | solution.py:238
  46.2 101.9 %copy-start.41 = (bf16[1024,128]{1,0:T(8,128)(2,1)}, bf16[1024,128]{1,0:T(8,128)(2,1)S(1)}, u32[]{:S(2)}) copy-start(bf16[1024,128]{1,0:T(8,128)(2,1)S(1)} %all_gather.47) | copy-start | bytes 786436
  144.4 23.5 %copy-start.20 = (pred[512,1024]{1,0:T(8,128)(4,1)}, pred[512,1024]{1,0:T(8,128)(4,1)S(1)}, u32[]{:S(2)}) copy-start(pred[512,1024]{1,0:T(8,128)(4,1)S(1)} %get-tuple-element.254) | copy-start | bytes 1572868
  144.5 39.0 %copy-start.18 = (pred[512,1024]{1,0:T(8,128)(4,1)}, pred[512,1024]{1,0:T(8,128)(4,1)S(1)}, u32[]{:S(2)}) copy-start(pred[512,1024]{1,0:T(8,128)(4,1)S(1)} %get-tuple-element.253) | copy-start | bytes 1572868
  173.6 91.0 %reduce-scatter.16.cloned.1.call-start = ((), (), s32[]{:S(2)}) async-start(), calls=%async_computation.16 | async-start | bytes 5242880 | tf_op jit(solution)/shard_map/reduce_scatter | solution.py:238
  190.3 74.3 %copy-start.14 = (bf16[2,1,256,1024]{3,2,1,0:T(8,128)(2,1)S(1)}, bf16[2,1,256,1024]{3,2,1,0:T(8,128)(2,1)}, u32[]{:S(2)}) copy-start(bf16[2,1,256,1024]{3,2,1,0:T(8,128)(2,1)} %param.38) | copy-start | bytes 3145732
  190.3 76.2 %copy-start.95 = (f32[1024]{0:T(1024)S(1)}, f32[1024]{0:T(1024)}, u32[]{:S(2)}) copy-start(f32[1024]{0:T(1024)} %param.47) | copy-start | bytes 12292
  190.3 81.4 %all-gather.18.cloned.1.call-start = ((), (), s32[]{:S(2)}) async-start(), calls=%async_computation.18 | async-start | bytes 2654208 | tf_op jit(solution)/shard_map/all_gather | solution.py:97
  190.9 99.3 %all-gather.16.cloned.1.call-start = ((), (), s32[]{:S(2)}) async-start(), calls=%async_computation.17 | async-start | bytes 2621440 | tf_op jit(solution)/shard_map/all_gather | solution.py:243
  266.5 336.3 %copy-start.16 = (f32[256,1024]{1,0:T(8,128)}, f32[256,1024]{1,0:T(8,128)S(1)}, u32[]{:S(2)}) copy-start(f32[256,1024]{1,0:T(8,128)S(1)} %get-tuple-element.188) | copy-start | bytes 3145732
  267.6 76.3 %all-gather.20.cloned.1.call-start = ((), (), s32[]{:S(2)}) async-start(), calls=%async_computation.19 | async-start | bytes 2654208 | tf_op jit(solution)/shard_map/all_gather | solution.py:98
  268.2 98.9 %all-gather.32.cloned.1.call-start = ((), (), s32[]{:S(2)}) async-start(), calls=%async_computation.39 | async-start | bytes 2621440 | tf_op jit(solution)/shard_map/all_gather | solution.py:259
  270.5 151.9 %all-gather.22.cloned.1.call-start = ((), (), s32[]{:S(2)}) async-start(), calls=%async_computation.20 | async-start | bytes 2654208 | tf_op jit(solution)/shard_map/all_gather | solution.py:99
  271.3 198.9 %reduce-scatter.24.cloned.1.call-start = ((), (), s32[]{:S(2)}) async-start(), calls=%async_computation.26 | async-start | bytes 2621440 | tf_op jit(solution)/shard_map/reduce_scatter | solution.py:266
  440.8 54.9 %all-gather.26.cloned.1.call-start = ((), (), s32[]{:S(2)}) async-start(), calls=%async_computation.24 | async-start | bytes 2621440 | tf_op jit(solution)/shard_map/all_gather | solution.py:243
  473.2 46.4 %all-gather.34.cloned.1.call-start = ((), (), s32[]{:S(2)}) async-start(), calls=%async_computation.40 | async-start | bytes 2621440 | tf_op jit(solution)/shard_map/all_gather | solution.py:259
  473.8 95.4 %reduce-scatter.28.cloned.1.call-start = ((), (), s32[]{:S(2)}) async-start(), calls=%async_computation.29 | async-start | bytes 2621440 | tf_op jit(solution)/shard_map/reduce_scatter | solution.py:266
  537.9 64.9 %reduce-scatter.22.cloned.1.call-start = ((), (), s32[]{:S(2)}) async-start(), calls=%async_computation.25 | async-start | bytes 2621440 | tf_op jit(solution)/shard_map/reduce_scatter | solution.py:250
  544.5 58.3 %copy-start.29 = (bf16[2,1,256,1024]{3,2,1,0:T(8,128)(2,1)S(1)}, bf16[2,1,256,1024]{3,2,1,0:T(8,128)(2,1)}, u32[]{:S(2)}) copy-start(bf16[2,1,256,1024]{3,2,1,0:T(8,128)(2,1)} %param.51) | copy-start | bytes 3145732
  544.6 83.9 %all-gather.30.cloned.1.call-start = ((), (), s32[]{:S(2)}) async-start(), calls=%async_computation.30 | async-start | bytes 2621440 | tf_op jit(solution)/shard_map/all_gather | solution.py:272
  544.8 61.9 %copy-start.124 = (f32[64]{0:T(128)S(1)}, f32[64]{0:T(128)}, u32[]{:S(2)}) copy-start(f32[64]{0:T(128)} %param.42) | copy-start | bytes 772
  544.9 62.0 %copy-start.122 = (f32[64]{0:T(128)S(1)}, f32[64]{0:T(128)}, u32[]{:S(2)}) copy-start(f32[64]{0:T(128)} %param.41) | copy-start | bytes 772
  544.9 62.1 %copy-start.108 = (f32[2,2,512]{2,1,0:T(2,128)S(1)}, f32[2,2,512]{2,1,0:T(2,128)}, u32[]{:S(2)}) copy-start(f32[2,2,512]{2,1,0:T(2,128)} %copy-done.107) | copy-start | bytes 24580
  544.9 62.1 %copy-start.101 = (f32[2,2,512]{2,1,0:T(2,128)S(1)}, f32[2,2,512]{2,1,0:T(2,128)}, u32[]{:S(2)}) copy-start(f32[2,2,512]{2,1,0:T(2,128)} %copy-done.100) | copy-start | bytes 24580
  544.9 62.1 %copy-start.115 = (f32[2,2,512]{2,1,0:T(2,128)S(1)}, f32[2,2,512]{2,1,0:T(2,128)}, u32[]{:S(2)}) copy-start(f32[2,2,512]{2,1,0:T(2,128)} %copy-done.114) | copy-start | bytes 24580
  544.9 62.1 %copy-start.110 = (f32[2,2,512]{2,1,0:T(2,128)S(1)}, f32[2,2,512]{2,1,0:T(2,128)}, u32[]{:S(2)}) copy-start(f32[2,2,512]{2,1,0:T(2,128)} %copy-done.109) | copy-start | bytes 24580
  544.9 62.1 %copy-start.103 = (f32[2,2,512]{2,1,0:T(2,128)S(1)}, f32[2,2,512]{2,1,0:T(2,128)}, u32[]{:S(2)}) copy-start(f32[2,2,512]{2,1,0:T(2,128)} %copy-done.102) | copy-start | bytes 24580
  605.9 25.2 %copy-start.28 = (pred[512,512]{0,1:T(8,128)(4,1)S(1)}, pred[512,512]{0,1:T(8,128)(4,1)}, u32[]{:S(2)}) copy-start(pred[512,512]{0,1:T(8,128)(4,1)} %get-tuple-element.252) | copy-start | bytes 786436
  605.9 47.2 %all-gather.28.cloned.1.call-start = ((), (), s32[]{:S(2)}) async-start(), calls=%async_computation.27 | async-start | bytes 2621440 | tf_op jit(solution)/shard_map/all_gather | solution.py:272
  606.7 163.0 %reduce-scatter.30.cloned.1.call-start = ((), (), s32[]{:S(2)}) async-start(), calls=%async_computation.31 | async-start | bytes 2621440 | tf_op jit(solution)/shard_map/reduce_scatter | solution.py:296
  633.1 20.0 %copy-start.51 = (bf16[256,1024]{1,0:T(8,128)(2,1)S(1)}, bf16[256,1024]{1,0:T(8,128)(2,1)}, u32[]{:S(2)}) copy-start(bf16[256,1024]{1,0:T(8,128)(2,1)} %all_gather.49) | copy-start | bytes 1572868
  655.6 19.5 %copy-start.87 = (bf16[1024,256]{0,1:T(8,128)(2,1)}, bf16[1024,256]{0,1:T(8,128)(2,1)S(1)}, u32[]{:S(2)}) copy-start(bf16[1024,256]{0,1:T(8,128)(2,1)S(1)} %convolution_convert_fusion.3) | copy-start | bytes 1572868
  703.2 66.6 %reduce-scatter.26.cloned.1.call-start = ((), (), s32[]{:S(2)}) async-start(), calls=%async_computation.28 | async-start | bytes 2621440 | tf_op jit(solution)/shard_map/reduce_scatter | solution.py:296
  714.6 96.6 %reduce-scatter.18.cloned.1.call-start = ((), (), s32[]{:S(2)}) async-start(), calls=%async_computation.21 | async-start | bytes 2621440 | tf_op jit(solution)/shard_map/reduce_scatter | solution.py:250
  721.4 147.7 %reduce-scatter.36.cloned.1.call-start = ((), (), s32[]{:S(2)}) async-start(), calls=%async_computation.34 | async-start | bytes 589824 | tf_op jit(solution)/shard_map/reduce_scatter | solution.py:314
  725.7 209.0 %reduce-scatter.34.cloned.1.call-start = ((), (), s32[]{:S(2)}) async-start(), calls=%async_computation.33 | async-start | bytes 589824 | tf_op jit(solution)/shard_map/reduce_scatter | solution.py:313
  729.2 304.3 %reduce-scatter.42.cloned.1.call-start = ((), (), s32[]{:S(2)}) async-start(), calls=%async_computation.37 | async-start | bytes 5308416 | tf_op jit(solution)/shard_map/reduce_scatter | solution.py:317
  739.7 393.3 %reduce-scatter.40.cloned.1.call-start = ((), (), s32[]{:S(2)}) async-start(), calls=%async_computation.36 | async-start | bytes 5308416 | tf_op jit(solution)/shard_map/reduce_scatter | solution.py:316
  750.0 451.2 %reduce-scatter.38.cloned.1.call-start = ((), (), s32[]{:S(2)}) async-start(), calls=%async_computation.35 | async-start | bytes 1179648 | tf_op jit(solution)/shard_map/reduce_scatter | solution.py:315
  755.5 512.8 %reduce-scatter.32.cloned.1.call-start = ((), (), s32[]{:S(2)}) async-start(), calls=%async_computation.32 | async-start | bytes 1179648 | tf_op jit(solution)/shard_map/reduce_scatter | solution.py:312
  759.3 608.1 %reduce-scatter.44.cloned.1.call-start = ((), (), s32[]{:S(2)}) async-start(), calls=%async_computation.38 | async-start | bytes 5308416 | tf_op jit(solution)/shard_map/reduce_scatter | solution.py:318
  768.6 42.6 %copy-start.17 = (f32[256,1024]{1,0:T(8,128)S(1)}, f32[256,1024]{1,0:T(8,128)}, u32[]{:S(2)}) copy-start(f32[256,1024]{1,0:T(8,128)} %copy-done.16) | copy-start | bytes 3145732
  (127 other events, 475.2 us)
Sparse Core Ops, SparseCore 0:
  12.8 25.2 all-gather.23
  40.2 22.5 all-gather.13
  173.7 43.8 reduce-scatter.19
  220.0 44.5 reduce-scatter.15
  538.0 31.1 reduce-scatter.27
  571.6 31.1 reduce-scatter.21
  703.3 31.1 reduce-scatter.29
  737.6 31.1 reduce-scatter.25
  771.4 31.2 reduce-scatter.17
  806.4 62.6 reduce-scatter.35
  873.0 61.6 reduce-scatter.33
  938.8 94.6 reduce-scatter.41
  1037.6 95.2 reduce-scatter.39
  1136.8 64.3 reduce-scatter.37
  1205.0 63.2 reduce-scatter.31
  1272.4 94.9 reduce-scatter.43
Sparse Core Ops, SparseCore 1:
  193.0 50.8 all-gather.17
  267.7 22.4 all-gather.15
  292.2 51.7 all-gather.19
  346.1 20.9 all-gather.31
  369.2 53.3 all-gather.21
  440.9 29.3 reduce-scatter.23
  473.2 22.4 all-gather.25
  497.1 22.4 all-gather.33
  606.0 22.4 all-gather.29
  630.6 22.4 all-gather.27
where the time goes:
time: 1380 us; the launch traced here: 1370 us
  waiting for transfers between devices  922 us (67%)
  matrix products  194 us (14%)
  blocking collectives  167 us (12%)
  other arithmetic  56.2 us (4%)
  between operations  17.9 us (1%)
  local copies, waits for them, and re-layouts  15.6 us (1%)
    reduce_scatter x1, waiting for transfers between devices, shards(): lax.psum_scatter(grad_accs[4], 'dp', scatter_dimension=0, tiled=True)  99.5 us
    reduce_scatter x1, waiting for transfers between devices, shards(): lax.psum_scatter(grad_accs[6], 'dp', scatter_dimension=1, tiled=True)  99.1 us
    reduce_scatter x1, waiting for transfers between devices, shards(): lax.psum_scatter(grad_accs[5], 'dp', scatter_dimension=0, tiled=True)  98.7 us
    reduce_scatter x2, waiting for transfers between devices, shards(): lax.psum_scatter(product(attended_low, out_full), 'tensor', scatter_dimen...  73.7 us
    reduce_scatter x1, waiting for transfers between devices, shards(): lax.psum_scatter(grad_accs[3], 'dp', scatter_dimension=1, tiled=True)  68.3 us
    reduce_scatter x1, waiting for transfers between devices, shards(): lax.psum_scatter(grad_accs[0], 'dp', scatter_dimension=0, tiled=True)  67.1 us
    reduce_scatter x1, waiting for transfers between devices, shards(): lax.psum_scatter(grad_accs[1], 'dp', scatter_dimension=0, tiled=True)  65.6 us
    dot_general x14, matrix products, product(): return jnp.dot(left_side, right_side, preferred_element_type=jnp.float32)  58.3 us
  transfers between devices with their start and end apart: 26, of which 20 were waited for; matrix products, arithmetic and copies ran while one was open for 10% of the time, Pallas kernels for 0%

commit v1 on v0

--- a/solution.py
+++ b/solution.py
@@ -1,11 +1,232 @@
+import functools
+
 import jax
 import jax.numpy as jnp
 from jax import lax
+from jax.experimental import pallas as pl
+from jax.experimental.pallas import tpu as pltpu
 from jax.sharding import PartitionSpec as P
 
 D = 1024
 DH = 64
 BLOCK = 512
+MESH = pl.DeviceIdType.MESH
+VMEM_LIMIT = 64000 * 1024
+PIECES = 4
+
+
+def remote(src, dst, send_sem, recv_sem, dp, tensor):
+    return pltpu.make_async_remote_copy(
+        src_ref=src,
+        dst_ref=dst,
+        send_sem=send_sem,
+        recv_sem=recv_sem,
+        device_id=(dp, tensor),
+        device_id_type=MESH,
+    )
+
+
+def place(dp_size):
+    dp = lax.axis_index("dp")
+    tensor = lax.axis_index("tensor")
+    return dp, tensor, dp // 2, lax.rem(dp, 2), dp_size // 2
+
+
+def greet(dp_size):
+    dp, tensor, outer, inner, outer_size = place(dp_size)
+    barrier = pltpu.get_barrier_semaphore()
+
+    @pl.loop(1, outer_size)
+    def _(shift):
+        peer = lax.rem(outer + shift, outer_size) * 2 + inner
+        pl.semaphore_signal(barrier, inc=1, device_id=(peer, tensor), device_id_type=MESH)
+
+    pl.semaphore_signal(
+        barrier, inc=1, device_id=(outer * 2 + 1 - inner, tensor), device_id_type=MESH
+    )
+    pl.semaphore_wait(barrier, outer_size)
+
+
+def gather_kernel(dp_size, *refs):
+    shards = refs[:PIECES]
+    fulls = refs[PIECES : 2 * PIECES]
+    outer_send, outer_recv, inner_send, inner_recv = refs[2 * PIECES :]
+    dp, tensor, outer, inner, outer_size = place(dp_size)
+    rows = shards[0].shape[0]
+    other = outer * 2 + 1 - inner
+    greet(dp_size)
+
+    def at(full, index):
+        return full.at[pl.ds(pl.multiple_of(index * rows, rows), rows), :]
+
+    def outer_copy(piece, shift):
+        peer = lax.rem(outer + shift, outer_size) * 2 + inner
+        return remote(
+            shards[piece],
+            at(fulls[piece], dp),
+            outer_send.at[piece, shift],
+            outer_recv.at[piece, shift],
+            peer,
+            tensor,
+        )
+
+    def inner_copy(piece, shift):
+        source = lax.rem(outer - shift + outer_size, outer_size) * 2 + inner
+        return remote(
+            at(fulls[piece], source),
+            at(fulls[piece], source),
+            inner_send.at[piece, shift],
+            inner_recv.at[piece, shift],
+            other,
+            tensor,
+        )
+
+    for piece in range(PIECES):
+        at(fulls[piece], dp)[...] = shards[piece][...]
+
+        @pl.loop(1, outer_size)
+        def _(shift):
+            outer_copy(piece, shift).start()
+
+        remote(
+            shards[piece],
+            at(fulls[piece], dp),
+            inner_send.at[piece, 0],
+            inner_recv.at[piece, 0],
+            other,
+            tensor,
+        ).start()
+    for piece in range(PIECES):
+
+        @pl.loop(1, outer_size)
+        def _(shift):
+            outer_copy(piece, shift).wait_recv()
+            inner_copy(piece, shift).start()
+
+    for piece in range(PIECES):
+        inner_copy(piece, 0).wait()
+
+        @pl.loop(1, outer_size)
+        def _(shift):
+            outer_copy(piece, shift).wait_send()
+            inner_copy(piece, shift).wait()
+
+
+def gather_weights(dp_size, shards):
+    whole = pl.BlockSpec(memory_space=pltpu.VMEM)
+    sems = pltpu.SemaphoreType.DMA((PIECES, dp_size // 2))
+    return pl.pallas_call(
+        functools.partial(gather_kernel, dp_size),
+        out_shape=[
+            jax.ShapeDtypeStruct((s.shape[0] * dp_size, s.shape[1]), s.dtype) for s in shards
+        ],
+        in_specs=[whole] * PIECES,
+        out_specs=[whole] * PIECES,
+        scratch_shapes=[sems] * 4,
+        compiler_params=pltpu.CompilerParams(
+            collective_id=0, has_side_effects=True, vmem_limit_bytes=VMEM_LIMIT
+        ),
+        name="gather_weights",
+    )(*shards)
+
+
+def scatter_kernel(dp_size, *refs):
+    partials = refs[:PIECES]
+    outs = refs[PIECES : 2 * PIECES]
+    inner_bufs = refs[2 * PIECES : 3 * PIECES]
+    outer_out = refs[3 * PIECES : 4 * PIECES]
+    outer_in = refs[4 * PIECES : 5 * PIECES]
+    outer_send, outer_recv, inner_send, inner_recv = refs[5 * PIECES :]
+    dp, tensor, outer, inner, outer_size = place(dp_size)
+    rows = outs[0].shape[0]
+    other = outer * 2 + 1 - inner
+    greet(dp_size)
+
+    def at(full, index):
+        return full.at[pl.ds(pl.multiple_of(index * rows, rows), rows), :]
+
+    def inner_copy(piece, shift):
+        target = lax.rem(outer + shift, outer_size) * 2 + 1 - inner
+        return remote(
+            at(partials[piece], target),
+            inner_bufs[piece].at[shift],
+            inner_send.at[piece, shift],
+            inner_recv.at[piece, shift],
+            other,
+            tensor,
+        )
+
+    def outer_copy(piece, shift):
+        peer = lax.rem(outer + shift, outer_size) * 2 + inner
+        return remote(
+            outer_out[piece].at[shift],
+            outer_in[piece].at[shift],
+            outer_send.at[piece, shift],
+            outer_recv.at[piece, shift],
+            peer,
+            tensor,
+        )
+
+    for piece in range(PIECES):
+
+        @pl.loop(1, outer_size)
+        def _(shift):
+            inner_copy(piece, shift).start()
+
+        inner_copy(piece, 0).start()
+    for piece in range(PIECES):
+
+        @pl.loop(1, outer_size)
+        def _(shift):
+            inner_copy(piece, shift).wait_recv()
+            target = lax.rem(outer + shift, outer_size) * 2 + inner
+            outer_out[piece][shift] = (
+                at(partials[piece], target)[...].astype(jnp.float32)
+                + inner_bufs[piece][shift].astype(jnp.float32)
+            ).astype(jnp.bfloat16)
+            outer_copy(piece, shift).start()
+
+        inner_copy(piece, 0).wait_recv()
+        outs[piece][...] = at(partials[piece], dp)[...].astype(jnp.float32) + inner_bufs[piece][
+            0
+        ].astype(jnp.float32)
+    for piece in range(PIECES):
+
+        @pl.loop(1, outer_size)
+        def _(shift):
+            outer_copy(piece, shift).wait_recv()
+            outs[piece][...] += outer_in[piece][shift].astype(jnp.float32)
+
+    for piece in range(PIECES):
+        inner_copy(piece, 0).wait_send()
+
+        @pl.loop(1, outer_size)
+        def _(shift):
+            inner_copy(piece, shift).wait_send()
+            outer_copy(piece, shift).wait_send()
+
+
+def scatter_grads(dp_size, partials):
+    whole = pl.BlockSpec(memory_space=pltpu.VMEM)
+    sems = pltpu.SemaphoreType.DMA((PIECES, dp_size // 2))
+    bufs = [
+        pltpu.VMEM((dp_size // 2, p.shape[0] // dp_size, p.shape[1]), jnp.bfloat16)
+        for p in partials
+    ]
+    return pl.pallas_call(
+        functools.partial(scatter_kernel, dp_size),
+        out_shape=[
+            jax.ShapeDtypeStruct((p.shape[0] // dp_size, p.shape[1]), jnp.float32)
+            for p in partials
+        ],
+        in_specs=[whole] * PIECES,
+        out_specs=[whole] * PIECES,
+        scratch_shapes=bufs * 3 + [sems] * 4,
+        compiler_params=pltpu.CompilerParams(
+            collective_id=1, has_side_effects=True, vmem_limit_bytes=VMEM_LIMIT
+        ),
+        name="scatter_grads",
+    )(*partials)
 
 
 NORM_EPS = 1e-05
@@ -61,6 +282,7 @@
 
 
 def shards(
+    dp_size,
     tokens,
     segment_ids,
     attn_gain,
@@ -87,17 +309,20 @@
     cosine_heads = cosine_table[:, None, :]
     sine_heads = sine_table[:, None, :]
     positions = jnp.arange(length)
+    attn_full, gate_kept, up_kept, down_kept = gather_weights(
+        dp_size,
+        (jnp.concatenate([w_query, w_key, w_value, w_out.T], axis=1), w_gate, w_up, w_down.T),
+    )
+    query_end = w_query.shape[1]
+    key_end = query_end + w_key.shape[1]
+    value_end = key_end + w_value.shape[1]
     attn_kept = (
-        lax.all_gather(w_query, "dp", axis=0, tiled=True),
-        lax.all_gather(w_key, "dp", axis=0, tiled=True),
-        lax.all_gather(w_value, "dp", axis=0, tiled=True),
-        lax.all_gather(w_out, "dp", axis=1, tiled=True),
-    )
-    ffn_kept = (
-        lax.all_gather(w_gate, "dp", axis=0, tiled=True),
-        lax.all_gather(w_up, "dp", axis=0, tiled=True),
-        lax.all_gather(w_down, "dp", axis=1, tiled=True),
-    )
+        attn_full[:, :query_end],
+        attn_full[:, query_end:key_end],
+        attn_full[:, key_end:value_end],
+        attn_full[:, value_end:],
+    )
+    ffn_kept = (gate_kept, up_kept, down_kept)
 
     def attn_source():
         return attn_kept
@@ -171,10 +396,10 @@
         jnp.zeros((D, w_query.shape[1]), jnp.float32),
         jnp.zeros((D, w_key.shape[1]), jnp.float32),
         jnp.zeros((D, w_value.shape[1]), jnp.float32),
-        jnp.zeros((w_out.shape[0], D), jnp.float32),
+        jnp.zeros((D, w_out.shape[0]), jnp.float32),
         jnp.zeros((D, w_gate.shape[1]), jnp.float32),
         jnp.zeros((D, w_up.shape[1]), jnp.float32),
-        jnp.zeros((w_down.shape[0], D), jnp.float32),
+        jnp.zeros((D, w_down.shape[0]), jnp.float32),
     )
     shard_sums = None
     attn_gain_acc = jnp.zeros((D,), jnp.float32)
@@ -236,7 +461,7 @@
         log_totals = attention_log_totals
         attended_low = attended.astype(jnp.bfloat16)
         branch = lax.psum_scatter(
-            product(attended_low, out_full), "tensor", scatter_dimension=0, tiled=True
+            times_transposed(attended_low, out_full), "tensor", scatter_dimension=0, tiled=True
         )
         middle = rows_in + branch
         ffn_normed, inverse_two = norm_forward(middle, ffn_gain)
@@ -248,7 +473,7 @@
         gate_act = gate_proj * gate_sig
         hidden = (gate_act * up_proj).astype(jnp.bfloat16)
         ffn_out = lax.psum_scatter(
-            product(hidden, down_full).astype(jnp.bfloat16),
+            times_transposed(hidden, down_full).astype(jnp.bfloat16),
             "tensor",
             scatter_dimension=0,
             tiled=True,
@@ -257,7 +482,7 @@
         upstream = cotangent[micro_index, 0].astype(jnp.float32)
         gate_full, up_full, down_full = ffn_source()
         ffn_upstream = lax.all_gather(upstream.astype(jnp.bfloat16), "tensor", axis=0, tiled=True)
-        hidden_grad = times_transposed(ffn_upstream, down_full)
+        hidden_grad = product(ffn_upstream, down_full)
         gate_grad = (
             hidden_grad * up_proj * gate_sig * (1.0 + gate_proj * (1.0 - gate_sig))
         ).astype(jnp.bfloat16)
@@ -273,7 +498,7 @@
             middle_grad.astype(jnp.bfloat16), "tensor", axis=0, tiled=True
         )
         query_full, key_full, value_full, out_full = attn_source()
-        attended_grad = times_transposed(attn_upstream, out_full).astype(jnp.bfloat16)
+        attended_grad = product(attn_upstream, out_full).astype(jnp.bfloat16)
         rot_query_grad, key_rot_grad, value_grad = attention_backward(
             query_major, key_major, value_major, log_totals, heads_major(attended_grad), segments
         )
@@ -303,19 +528,23 @@
             grad_accs[0] + transposed_times(normed_all, query_grad),
             grad_accs[1] + transposed_times(normed_all, key_grad),
             grad_accs[2] + transposed_times(normed_all, value_grad_low),
-            grad_accs[3] + transposed_times(attended_low, attn_upstream),
+            grad_accs[3] + transposed_times(attn_upstream, attended_low),
             grad_accs[4] + transposed_times(ffn_all, gate_grad),
             grad_accs[5] + transposed_times(ffn_all, up_grad),
-            grad_accs[6] + transposed_times(hidden, ffn_upstream),
-        )
+            grad_accs[6] + transposed_times(ffn_upstream, hidden),
+        )
+    low_accs = [acc.astype(jnp.bfloat16) for acc in grad_accs]
+    attn_sum, gate_sum, up_sum, down_sum = scatter_grads(
+        dp_size, (jnp.concatenate(low_accs[:4], axis=1), *low_accs[4:])
+    )
     shard_sums = (
-        lax.psum_scatter(grad_accs[0], "dp", scatter_dimension=0, tiled=True),
-        lax.psum_scatter(grad_accs[1], "dp", scatter_dimension=0, tiled=True),
-        lax.psum_scatter(grad_accs[2], "dp", scatter_dimension=0, tiled=True),
-        lax.psum_scatter(grad_accs[3], "dp", scatter_dimension=1, tiled=True),
-        lax.psum_scatter(grad_accs[4], "dp", scatter_dimension=0, tiled=True),
-        lax.psum_scatter(grad_accs[5], "dp", scatter_dimension=0, tiled=True),
-        lax.psum_scatter(grad_accs[6], "dp", scatter_dimension=1, tiled=True),
+        attn_sum[:, :query_end],
+        attn_sum[:, query_end:key_end],
+        attn_sum[:, key_end:value_end],
+        attn_sum[:, value_end:].T,
+        gate_sum,
+        up_sum,
+        down_sum.T,
     )
     gain_sums = lax.psum(
         (attn_gain_acc, query_gain_acc, key_gain_acc, ffn_gain_acc), ("dp", "tensor")
@@ -357,7 +586,7 @@
         P(None, "dp", "tensor", None),
     )
     return jax.shard_map(
-        shards,
+        functools.partial(shards, mesh.shape["dp"]),
         mesh=mesh,
         in_specs=placed,
         out_specs=(

time: 1380 us -> 829 us (0.60)
  waiting for transfers between devices: 922 us -> 263 us
  Pallas kernels: 0 us -> 230 us
  blocking collectives: 167 us -> 38.8 us
  matrix products: 194 us -> 179 us
    reduce_scatter x11 -> x4, waiting for transfers between devices: 656 us -> 110 us  [the longest x2 78.7 us: shards(): lax.psum_scatter(times_transposed(attended_low, out_full), 'tensor', scat...]
    pallas_call x0 -> x2, Pallas kernels: none -> 230 us  [the longest x1 119 us: gather_weights(): pl.pallas_call(functools.partial(gather_kernel, dp_size), out_shape=[jax....]
    all_gather x4 -> x0, blocking collectives: 127 us -> none  [the longest x1 33.7 us: shards(): lax.all_gather(w_query, 'dp', axis=0, tiled=True)]
    all_gather x3 -> x0, waiting for transfers between devices: 102 us -> none  [the longest x1 55.4 us: shards(): lax.all_gather(w_down, 'dp', axis=1, tiled=True)]
    dot_general x14, matrix products: 45 us -> 30.4 us  [transposed_times(): lax.dot_general(left_side, right_side, (((0,), (0,)), ((), ())), preferre...]
  transfers between devices with their start and end apart: 26 -> 16, of which waited for: 20 -> 11; matrix products, arithmetic and copies ran while one was open for 10% -> 17% of each run, Pallas kernels for 0% -> 28%
where the time goes in v1:
time: 829 us; the launch traced here: 818 us
  waiting for transfers between devices  263 us (32%)
  Pallas kernels  230 us (28%)
  matrix products  179 us (22%)
  other arithmetic  64.8 us (8%)
  blocking collectives  38.8 us (5%)
  local copies, waits for them, and re-layouts  24.1 us (3%)
  between operations  16.6 us (2%)
    pallas_call x1, Pallas kernels, gather_weights(): pl.pallas_call(functools.partial(gather_kernel, dp_size), out_shape=[jax....  119 us
    pallas_call x1, Pallas kernels, scatter_grads(): pl.pallas_call(functools.partial(scatter_kernel, dp_size), out_shape=[jax...  111 us
    reduce_scatter x2, waiting for transfers between devices, shards(): lax.psum_scatter(times_transposed(attended_low, out_full), 'tensor', scat...  78.7 us
    dot_general x14, matrix products, product(): return jnp.dot(left_side, right_side, preferred_element_type=jnp.float32)  64.3 us
    reduce_scatter x2, waiting for transfers between devices, shards(): lax.psum_scatter(ffn_part.astype(jnp.bfloat16), 'tensor', scatter_dimensi...  54.2 us
    all_gather x2, waiting for transfers between devices, shards(): lax.all_gather(ffn_normed.astype(jnp.bfloat16), 'tensor', axis=0, tiled=T...  41.7 us
    dot_general x14, matrix products, times_transposed(): lax.dot_general(left_side, right_side, (((1,), (1,)), ((), ())), preferre...  41.4 us
    psum x1, blocking collectives, shards(): lax.psum((attn_gain_acc, query_gain_acc, key_gain_acc, ffn_gain_acc), ('d...  38.8 us
  transfers between devices with their start and end apart: 16, of which 11 were waited for; matrix products, arithmetic and copies ran while one was open for 17% of the time, Pallas kernels for 28%

profile of v1, /device:TPU:0, one launch (start us, length us, event | category | flops | bytes accessed | tf_op | source)
XLA Modules:
  0.0 818.2 jit_solution(10176949047875039943)
XLA Ops:
  14.0 119.1 %gather_weights.1 = (bf16[1024,768]{1,0:T(8,128)(2,1)}, bf16[1024,1152]{1,0:T(8,128)(2,1)}, bf16[1024,1152]{1,0:T(8,128)(2,1)}, bf16[1024,1152]{1,0:T(8,128)(2,1)}) custom-call(bf16[128,768]{1,0:T(8,128)(2,1)} %pad_maximum_fusion.9.refs_0_, bf16[128,1152]{1,0:T(8,128)(2,1)} %refs_1_.1, bf16[128,1152]{1,0:T(8,128)(2,1)} %refs_2_.1, bf16[128,1152]{1,0:T(8,128)(2,1)} %bitcast.447), custom_call_target="tpu_custom_call" | custom-call | tf_op jit(solution)/shard_map/gather_weights/pallas_call | solution.py:118
  136.6 3.6 multiply_reduce_fusion.12
  140.3 2.6 multiply_reduce_fusion.13
  142.9 2.7 multiply_reduce_fusion.7
  161.6 2.6 fusion.82
  165.1 2.8 fusion.136
  178.1 2.6 fusion.83
  180.9 4.2 fusion.138
  185.1 31.7 %reduce-scatter.13.cloned.1.call-done = f32[256,1024]{1,0:T(8,128)} async-done(((f32[1024,1024]{1,0:T(8,128)}), f32[256,1024]{1,0:T(8,128)}) %reduce-scatter.13.cloned.1.call-update) | async-done | bytes 1048592 | tf_op jit(solution)/shard_map/reduce_scatter | solution.py:463
  216.8 47.0 %reduce-scatter.9.cloned.1.call-done = f32[256,1024]{1,0:T(8,128)} async-done(((f32[1024,1024]{1,0:T(8,128)}), f32[256,1024]{1,0:T(8,128)}) %reduce-scatter.9.cloned.1.call-update) | async-done | bytes 1048592 | tf_op jit(solution)/shard_map/reduce_scatter | solution.py:463
  270.0 20.2 %all-gather.13.cloned.1.call-done = bf16[1024,1024]{1,0:T(8,128)(2,1)} async-done(((bf16[256,1024]{1,0:T(8,128)(2,1)}), bf16[1024,1024]{1,0:T(8,128)(2,1)}) %all-gather.13.cloned.1.call-update) | async-done | bytes 2097168 | tf_op jit(solution)/shard_map/all_gather | solution.py:468
  290.2 7.5 fusion.216
  297.7 4.5 fusion.215
  302.2 12.6 %all-gather.23.cloned.1.call-done = bf16[1,1,1024,1024]{3,2,1,0:T(8,128)(2,1)} async-done(((bf16[1,1,256,1024]{3,2,1,0:T(8,128)(2,1)}), bf16[1,1,1024,1024]{3,2,1,0:T(8,128)(2,1)}) %all-gather.23.cloned.1.call-update) | async-done | bytes 2097168 | tf_op jit(solution)/shard_map/all_gather | solution.py:484
  314.8 10.8 %fusion.11 = (bf16[1024,1152]{1,0:T(8,128)(2,1)S(1)}, bf16[1024,1152]{1,0:T(8,128)(2,1)S(1)}, bf16[1024,1152]{1,0:T(8,128)(2,1)}) fusion(f32[1024,1152]{1,0:T(8,128)} %fusion.215, f32[1024,1152]{1,0:T(8,128)} %fusion.216, bf16[1024,1152]{1,0:T(8,128)(2,1)} %get-tuple-element.152, bf16[1,1,1024,1024]{3,2,1,0:T(8,128)(2,1)} %all-gather.23.cloned.1.call-done), kind=kOutput, calls=%fused_computation.27 | convolution fusion | flops 2433613824 | bytes 20971520 | tf_op jit(solution)/shard_map/dot_general | solution.py:269
  325.6 2.9 fusion.219
  328.9 4.1 add_convert_fusion.6
  333.1 31.3 %reduce-scatter.17.cloned.1.call-done = bf16[256,1024]{1,0:T(8,128)(2,1)} async-done(((bf16[1024,1024]{1,0:T(8,128)(2,1)}), bf16[256,1024]{1,0:T(8,128)(2,1)}) %reduce-scatter.17.cloned.1.call-update) | async-done | bytes 524304 | tf_op jit(solution)/shard_map/reduce_scatter | solution.py:491
  364.4 2.9 fusion.106
  368.5 21.5 %all-gather.17.cloned.1.call-done = bf16[1024,1024]{1,0:T(8,128)(2,1)} async-done(((bf16[256,1024]{1,0:T(8,128)(2,1)}), bf16[1024,1024]{1,0:T(8,128)(2,1)}) %all-gather.17.cloned.1.call-update) | async-done | bytes 2097168 | tf_op jit(solution)/shard_map/all_gather | solution.py:468
  390.0 7.5 fusion.218
  397.6 4.5 fusion.217
  402.0 12.1 %all-gather.25.cloned.1.call-done = bf16[1,1,1024,1024]{3,2,1,0:T(8,128)(2,1)} async-done(((bf16[1,1,256,1024]{3,2,1,0:T(8,128)(2,1)}), bf16[1,1,1024,1024]{3,2,1,0:T(8,128)(2,1)}) %all-gather.25.cloned.1.call-update) | async-done | bytes 2097168 | tf_op jit(solution)/shard_map/all_gather | solution.py:484
  414.2 10.8 %fusion.7 = (bf16[1024,1152]{1,0:T(8,128)(2,1)S(1)}, bf16[1024,1152]{1,0:T(8,128)(2,1)S(1)}, bf16[1024,1152]{1,0:T(8,128)(2,1)}) fusion(f32[1024,1152]{1,0:T(8,128)} %fusion.217, f32[1024,1152]{1,0:T(8,128)} %fusion.218, bf16[1024,1152]{1,0:T(8,128)(2,1)} %get-tuple-element.152, bf16[1,1,1024,1024]{3,2,1,0:T(8,128)(2,1)} %all-gather.25.cloned.1.call-done), kind=kOutput, calls=%fused_computation.21 | convolution fusion | flops 2433613824 | bytes 20971520 | tf_op jit(solution)/shard_map/dot_general | solution.py:269
  425.0 2.9 fusion.220
  428.4 4.1 add_convert_fusion.4
  432.5 6.6 convolution_convert_fusion
  440.9 22.9 %reduce-scatter.21.cloned.1.call-done = bf16[256,1024]{1,0:T(8,128)(2,1)} async-done(((bf16[1024,1024]{1,0:T(8,128)(2,1)}), bf16[256,1024]{1,0:T(8,128)(2,1)}) %reduce-scatter.21.cloned.1.call-update) | async-done | bytes 524304 | tf_op jit(solution)/shard_map/reduce_scatter | solution.py:491
  466.5 31.1 %reduce-scatter.15.cloned.1.call-done = bf16[256,1024]{1,0:T(8,128)(2,1)} async-done(((bf16[1024,1024]{1,0:T(8,128)(2,1)}), bf16[256,1024]{1,0:T(8,128)(2,1)}) %reduce-scatter.15.cloned.1.call-update) | async-done | bytes 524304 | tf_op jit(solution)/shard_map/reduce_scatter | solution.py:475
  497.6 3.1 fusion.209
  507.6 15.8 %all-gather.19.cloned.1.call-done = bf16[1024,1024]{1,0:T(8,128)(2,1)} async-done(((bf16[256,1024]{1,0:T(8,128)(2,1)}), bf16[1024,1024]{1,0:T(8,128)(2,1)}) %all-gather.19.cloned.1.call-update) | async-done | bytes 2097168 | tf_op jit(solution)/shard_map/all_gather | solution.py:497
  525.9 3.7 multiply_reduce_fusion.3
  533.7 14.4 %all-gather.21.cloned.1.call-done = bf16[1024,1024]{1,0:T(8,128)(2,1)} async-done(((bf16[256,1024]{1,0:T(8,128)(2,1)}), bf16[1024,1024]{1,0:T(8,128)(2,1)}) %all-gather.21.cloned.1.call-update) | async-done | bytes 2097168 | tf_op jit(solution)/shard_map/all_gather | solution.py:497
  550.7 3.0 fusion.91
  559.3 5.4 multiply_reduce_fusion
  567.2 4.7 multiply_convert_fusion
  574.6 3.0 multiply_reduce_fusion.1
  577.6 2.6 multiply_convert_fusion.1
  603.2 6.8 convolution_convert_fusion.1
  610.1 4.9 fusion.30
  615.0 3.0 fusion.226
  618.1 3.1 fusion.225
  621.2 4.6 fusion.24.refs_3_
  625.8 4.3 add_convert_fusion.1.refs_2_
  630.1 4.4 add_convert_fusion.2.refs_1_
  643.4 111.2 %scatter_grads.1 = (f32[128,768]{1,0:T(8,128)}, f32[128,1152]{1,0:T(8,128)}, f32[128,1152]{1,0:T(8,128)}, f32[128,1152]{1,0:T(8,128)}) custom-call(bf16[1024,768]{1,0:T(8,128)(2,1)} %pad_maximum_fusion.refs_0_, bf16[1024,1152]{1,0:T(8,128)(2,1)} %add_convert_fusion.2.refs_1_, bf16[1024,1152]{1,0:T(8,128)(2,1)} %add_convert_fusion.1.refs_2_, ...), custom_call_target="tpu_custom_call" | custom-call | tf_op jit(solution)/shard_map/scatter_grads/pallas_call | solution.py:216
  762.9 3.2 fusion.96
  770.8 38.8 %all-reduce.4 = (f32[1024]{0:T(1024)}, f32[64]{0:T(128)}, f32[64]{0:T(128)}, f32[1024]{0:T(1024)}) all-reduce(f32[1024]{0:T(1024)S(1)} %add.338, f32[64]{0:T(128)S(1)} %add.339, f32[64]{0:T(128)S(1)} %add.340, f32[1024]{0:T(1024)S(1)} %add.348), channel_id=1, replica_groups=mesh['dp'=8,'tensor'=4] {'dp','tensor'}, use_global_device_ids=true, to_apply=%region_38.39 | all-reduce | flops 2176 | bytes 17408 | tf_op jit(solution)/shard_map/psum | solution.py:549
  (480 shorter events, 121.9 us)
Async XLA Ops:
  7.2 125.8 %copy-start.108 = (s32[2,1,1024]{2,1,0:T(1,128)S(1)}, s32[2,1,1024]{2,1,0:T(1,128)}, u32[]{:S(2)}) copy-start(s32[2,1,1024]{2,1,0:T(1,128)} %param.39) | copy-start | bytes 24580
  7.2 129.4 %all-gather.15.cloned.1.call-start = ((), (), s32[]{:S(2)}) async-start(), calls=%async_computation.12 | async-start | bytes 2621440 | tf_op jit(solution)/shard_map/all_gather | solution.py:416
  11.4 128.8 %all-gather.11.cloned.1.call-start = ((), (), s32[]{:S(2)}) async-start(), calls=%async_computation.8 | async-start | bytes 2621440 | tf_op jit(solution)/shard_map/all_gather | solution.py:416
  12.2 204.7 %reduce-scatter.13.cloned.1.call-start = ((), (), s32[]{:S(2)}) async-start(), calls=%async_computation.13 | async-start | bytes 5242880 | tf_op jit(solution)/shard_map/reduce_scatter | solution.py:463
  134.4 15.3 %copy-start.44 = (f32[1024,32]{0,1:T(8,128)}, f32[1024,32]{0,1:T(8,128)S(1)}, u32[]{:S(2)}) copy-start(f32[1024,32]{0,1:T(8,128)S(1)} %get-tuple-element.277) | copy-start | bytes 393220
  136.6 25.0 %copy-start.18 = (pred[512,1024]{1,0:T(8,128)(4,1)}, pred[512,1024]{1,0:T(8,128)(4,1)S(1)}, u32[]{:S(2)}) copy-start(pred[512,1024]{1,0:T(8,128)(4,1)S(1)} %get-tuple-element.274) | copy-start | bytes 1572868
  136.6 41.5 %copy-start.16 = (pred[512,1024]{1,0:T(8,128)(4,1)}, pred[512,1024]{1,0:T(8,128)(4,1)S(1)}, u32[]{:S(2)}) copy-start(pred[512,1024]{1,0:T(8,128)(4,1)S(1)} %get-tuple-element.273) | copy-start | bytes 1572868
  152.6 9.0 %copy-start.1 = (f32[2,2,512,1024]{3,2,1,0:T(8,128)}, f32[2,2,512,1024]{3,2,1,0:T(8,128)S(1)}, u32[]{:S(2)}) copy-start(f32[2,2,512,1024]{3,2,1,0:T(8,128)S(1)} %get-tuple-element.295) | copy-start | bytes 25165828
  152.6 9.0 %copy-start.99 = (f32[2,2,512]{2,1,0:T(2,128)}, f32[2,2,512]{2,1,0:T(2,128)S(1)}, u32[]{:S(2)}) copy-start(f32[2,2,512]{2,1,0:T(2,128)S(1)} %get-tuple-element.294) | copy-start | bytes 24580
  167.9 96.0 %reduce-scatter.9.cloned.1.call-start = ((), (), s32[]{:S(2)}) async-start(), calls=%async_computation.9 | async-start | bytes 5242880 | tf_op jit(solution)/shard_map/reduce_scatter | solution.py:463
  180.9 83.0 %copy-start.11 = (bf16[2,1,256,1024]{3,2,1,0:T(8,128)(2,1)S(1)}, bf16[2,1,256,1024]{3,2,1,0:T(8,128)(2,1)}, u32[]{:S(2)}) copy-start(bf16[2,1,256,1024]{3,2,1,0:T(8,128)(2,1)} %param.38) | copy-start | bytes 3145732
  185.0 81.3 %copy-start.89 = (f32[1024]{0:T(1024)S(1)}, f32[1024]{0:T(1024)}, u32[]{:S(2)}) copy-start(f32[1024]{0:T(1024)} %param.47) | copy-start | bytes 12292
  185.1 105.1 %all-gather.13.cloned.1.call-start = ((), (), s32[]{:S(2)}) async-start(), calls=%async_computation.10 | async-start | bytes 2621440 | tf_op jit(solution)/shard_map/all_gather | solution.py:468
  266.3 231.3 %copy-start.13 = (f32[256,1024]{1,0:T(8,128)}, f32[256,1024]{1,0:T(8,128)S(1)}, u32[]{:S(2)}) copy-start(f32[256,1024]{1,0:T(8,128)S(1)} %get-tuple-element.204) | copy-start | bytes 3145732
  266.3 231.3 %copy-start.15 = (f32[256,1024]{1,0:T(8,128)}, f32[256,1024]{1,0:T(8,128)S(1)}, u32[]{:S(2)}) copy-start(f32[256,1024]{1,0:T(8,128)S(1)} %get-tuple-element.241) | copy-start | bytes 3145732
  266.3 98.1 %copy-start.111 = (f32[256]{0:T(256)}, f32[256]{0:T(256)S(1)}, u32[]{:S(2)}) copy-start(f32[256]{0:T(256)S(1)} %add_rsqrt_fusion.6) | copy-start | bytes 3076
  267.4 47.3 %all-gather.23.cloned.1.call-start = ((), (), s32[]{:S(2)}) async-start(), calls=%async_computation.22 | async-start | bytes 2621440 | tf_op jit(solution)/shard_map/all_gather | solution.py:484
  269.7 94.6 %reduce-scatter.17.cloned.1.call-start = ((), (), s32[]{:S(2)}) async-start(), calls=%async_computation.16 | async-start | bytes 2621440 | tf_op jit(solution)/shard_map/reduce_scatter | solution.py:491
  314.8 10.8 %copy-start.131 = (bf16[1024,1152]{1,0:T(8,128)(2,1)S(1)}, bf16[1024,1152]{1,0:T(8,128)(2,1)}, u32[]{:S(2)}) copy-start(bf16[1024,1152]{1,0:T(8,128)(2,1)} %get-tuple-element.150) | copy-start | bytes 7077892
  333.0 57.0 %all-gather.17.cloned.1.call-start = ((), (), s32[]{:S(2)}) async-start(), calls=%async_computation.14 | async-start | bytes 2621440 | tf_op jit(solution)/shard_map/all_gather | solution.py:468
  367.3 46.9 %all-gather.25.cloned.1.call-start = ((), (), s32[]{:S(2)}) async-start(), calls=%async_computation.23 | async-start | bytes 2621440 | tf_op jit(solution)/shard_map/all_gather | solution.py:484
  368.0 95.8 %reduce-scatter.21.cloned.1.call-start = ((), (), s32[]{:S(2)}) async-start(), calls=%async_computation.19 | async-start | bytes 2621440 | tf_op jit(solution)/shard_map/reduce_scatter | solution.py:491
  414.2 10.8 %copy-start.133 = (bf16[1024,1152]{1,0:T(8,128)(2,1)S(1)}, bf16[1024,1152]{1,0:T(8,128)(2,1)}, u32[]{:S(2)}) copy-start(bf16[1024,1152]{1,0:T(8,128)(2,1)} %get-tuple-element.150) | copy-start | bytes 7077892
  432.5 65.1 %reduce-scatter.15.cloned.1.call-start = ((), (), s32[]{:S(2)}) async-start(), calls=%async_computation.15 | async-start | bytes 2621440 | tf_op jit(solution)/shard_map/reduce_scatter | solution.py:475
  439.2 58.4 %copy-start.28 = (bf16[2,1,256,1024]{3,2,1,0:T(8,128)(2,1)S(1)}, bf16[2,1,256,1024]{3,2,1,0:T(8,128)(2,1)}, u32[]{:S(2)}) copy-start(bf16[2,1,256,1024]{3,2,1,0:T(8,128)(2,1)} %param.51) | copy-start | bytes 3145732
  439.2 84.2 %all-gather.19.cloned.1.call-start = ((), (), s32[]{:S(2)}) async-start(), calls=%async_computation.17 | async-start | bytes 2621440 | tf_op jit(solution)/shard_map/all_gather | solution.py:497
  500.7 25.2 %copy-start.68 = (bf16[1024,128]{0,1:T(8,128)(2,1)S(1)}, bf16[1024,128]{0,1:T(8,128)(2,1)}, u32[]{:S(2)}) copy-start(bf16[1024,128]{0,1:T(8,128)(2,1)} %copy-done.67) | copy-start | bytes 786436
  500.7 47.4 %all-gather.21.cloned.1.call-start = ((), (), s32[]{:S(2)}) async-start(), calls=%async_computation.20 | async-start | bytes 2621440 | tf_op jit(solution)/shard_map/all_gather | solution.py:497
  501.5 259.4 %reduce-scatter.23.cloned.1.call-start = ((), (), s32[]{:S(2)}) async-start(), calls=%async_computation.21 | async-start | bytes 2621440 | tf_op jit(solution)/shard_map/reduce_scatter | solution.py:521
  504.8 48.9 %copy-start.98 = (f32[2,2,512]{2,1,0:T(2,128)}, f32[2,2,512]{2,1,0:T(2,128)S(1)}, u32[]{:S(2)}) copy-start(f32[2,2,512]{2,1,0:T(2,128)S(1)} %log_add_fusion.1) | copy-start | bytes 24580
  505.5 24.1 %copy-start.96 = (f32[2,2,512]{2,1,0:T(2,128)}, f32[2,2,512]{2,1,0:T(2,128)S(1)}, u32[]{:S(2)}) copy-start(f32[2,2,512]{2,1,0:T(2,128)S(1)} %log_add_fusion.3) | copy-start | bytes 24580
  531.0 17.2 %copy-start.23 = (bf16[1024,768]{1,0:T(8,128)(2,1)S(1)}, bf16[1024,768]{1,0:T(8,128)(2,1)}, u32[]{:S(2)}) copy-start(bf16[1024,768]{1,0:T(8,128)(2,1)} %get-tuple-element.149) | copy-start | bytes 4718596
  531.0 19.7 %copy-start.21 = (pred[512,512]{0,1:T(8,128)(4,1)S(1)}, pred[512,512]{0,1:T(8,128)(4,1)}, u32[]{:S(2)}) copy-start(pred[512,512]{0,1:T(8,128)(4,1)} %get-tuple-element.272) | copy-start | bytes 786436
  533.7 20.0 %copy-start.66 = (bf16[1024,128]{0,1:T(8,128)(2,1)S(1)}, bf16[1024,128]{0,1:T(8,128)(2,1)}, u32[]{:S(2)}) copy-start(bf16[1024,128]{0,1:T(8,128)(2,1)} %copy-done.65) | copy-start | bytes 786436
  564.7 9.5 %slice-start = ((s8[8388608]{0:T(1024)(128)(4,1)}), s8[4194304]{0:T(1024)(128)(4,1)S(1)}, s32[]{:S(2)}) async-start(s8[8388608]{0:T(1024)(128)(4,1)} %bitcast.423), calls=%async_computation.24 | async-start | bytes 8388608
  591.9 168.9 %reduce-scatter.19.cloned.1.call-start = ((), (), s32[]{:S(2)}) async-start(), calls=%async_computation.18 | async-start | bytes 2621440 | tf_op jit(solution)/shard_map/reduce_scatter | solution.py:521
  603.0 163.1 %reduce-scatter.11.cloned.1.call-start = ((), (), s32[]{:S(2)}) async-start(), calls=%async_computation.11 | async-start | bytes 2621440 | tf_op jit(solution)/shard_map/reduce_scatter | solution.py:475
  643.4 117.5 %copy-start.12 = (bf16[2,1,256,1024]{3,2,1,0:T(8,128)(2,1)S(1)}, bf16[2,1,256,1024]{3,2,1,0:T(8,128)(2,1)}, u32[]{:S(2)}) copy-start(bf16[2,1,256,1024]{3,2,1,0:T(8,128)(2,1)} %param.38) | copy-start | bytes 3145732
  643.4 117.5 %copy-start.103 = (f32[1024]{0:T(1024)S(1)}, f32[1024]{0:T(1024)}, u32[]{:S(2)}) copy-start(f32[1024]{0:T(1024)} %param.40) | copy-start | bytes 12292
  643.4 117.5 %copy-start.114 = (f32[256]{0:T(256)S(1)}, f32[256]{0:T(256)}, u32[]{:S(2)}) copy-start(f32[256]{0:T(256)} %copy-done.113) | copy-start | bytes 3076
  643.4 117.5 %copy-start.116 = (f32[256]{0:T(256)S(1)}, f32[256]{0:T(256)}, u32[]{:S(2)}) copy-start(f32[256]{0:T(256)} %copy-done.115) | copy-start | bytes 3076
  754.6 8.2 %copy-start.121 = (f32[256]{0:T(256)S(1)}, f32[256]{0:T(256)}, u32[]{:S(2)}) copy-start(f32[256]{0:T(256)} %broadcast_multiply_fusion.5) | copy-start | bytes 3076
  754.6 11.5 %copy-start.14 = (f32[256,1024]{1,0:T(8,128)S(1)}, f32[256,1024]{1,0:T(8,128)}, u32[]{:S(2)}) copy-start(f32[256,1024]{1,0:T(8,128)} %copy-done.13) | copy-start | bytes 3145732
  754.6 11.5 %copy-start.37 = (bf16[256,1024]{1,0:T(8,128)(2,1)S(1)}, bf16[256,1024]{1,0:T(8,128)(2,1)}, u32[]{:S(2)}) copy-start(bf16[256,1024]{1,0:T(8,128)(2,1)} %reduce-scatter.17.cloned.1.call-done) | copy-start | bytes 1572868
  754.6 11.5 %copy-start.112 = (f32[256]{0:T(256)S(1)}, f32[256]{0:T(256)}, u32[]{:S(2)}) copy-start(f32[256]{0:T(256)} %copy-done.111) | copy-start | bytes 3076
  754.6 11.5 %copy-start.120 = (f32[256]{0:T(256)S(1)}, f32[256]{0:T(256)}, u32[]{:S(2)}) copy-start(f32[256]{0:T(256)} %broadcast_multiply_fusion.7) | copy-start | bytes 3076
  768.3 41.4 %copy-start.80 = (f32[128,1152]{1,0:T(8,128)S(1)}, f32[128,1152]{1,0:T(8,128)}, u32[]{:S(2)}) copy-start(f32[128,1152]{1,0:T(8,128)} %get-tuple-element.331) | copy-start | bytes 1769476
  768.3 42.2 %copy-start.79 = (f32[128,1152]{1,0:T(8,128)S(1)}, f32[128,1152]{1,0:T(8,128)}, u32[]{:S(2)}) copy-start(f32[128,1152]{1,0:T(8,128)} %get-tuple-element.332) | copy-start | bytes 1769476
  (124 other events, 404.4 us)
Sparse Core Ops, SparseCore 0:
  11.5 25.2 all-gather.14
  39.0 22.5 all-gather.10
  168.0 48.8 reduce-scatter.12
  219.2 44.5 reduce-scatter.8
  267.6 22.5 all-gather.12
  292.2 22.5 all-gather.22
  333.1 31.1 reduce-scatter.16
  367.4 22.5 all-gather.16
  391.6 22.5 all-gather.24
  432.6 31.1 reduce-scatter.20
  466.4 31.1 reduce-scatter.14
  500.8 22.5 all-gather.18
  525.6 22.5 all-gather.20
  592.0 31.2 reduce-scatter.22
  626.3 31.1 reduce-scatter.18
  659.8 31.1 reduce-scatter.10
